TPU v7x, 128 devices: a whole 4x4x4 slice. The times are simulated.
128 devices in a mesh: tables: 1, g: 128 (over z, y, x, core).
Axes of the slice: x: 4, y: 4, z: 4, core: 2. Of those that a mesh axis runs over, the one named last changes fastest.
Arguments:
- item_factors: float32 [262144, 64], P(('tables', 'g'))
- user_start: float32 [65536, 64], P(('tables', 'g'))
- by_item_idx: int32 [128, 65536, 8], P(('tables', 'g'))
- by_item_conf: float32 [128, 65536, 8], P(('tables', 'g'))
- by_user_idx: int32 [128, 262144, 2], P(('tables', 'g'))
- by_user_conf: float32 [128, 262144, 2], P(('tables', 'g'))
Outputs:
- output 1: float32 [65536, 64], P(('tables', 'g'))
- output 2: float32 [262144, 64], P(('tables', 'g'))
All inputs are finite; a program needn't handle non-finite values.
Results may differ from a plain program's by a relative error of at most 0.0123.
Values are sent between devices in bfloat16 or wider.
A program may use at most 1 GiB of HBM per device.

v0:
```python
import functools

import jax
import jax.numpy as jnp
from jax import lax
from jax.experimental import pallas as pl
from jax.experimental.pallas import tpu as pltpu
from jax.sharding import PartitionSpec as P


REG_LAMBDA = 0.01
CG_STEPS = 3
F = 64
FX = F + 16
PITCH = F + 8
LN = 128
G = 128
PAY = 48
EMPTY = 2048
PACK = 4096
F32 = jnp.float32
BF16 = jnp.bfloat16
I16 = jnp.int16
I32 = jnp.int32


def iota(shape, dim, dtype=I32):
    return lax.broadcasted_iota(dtype, shape, dim)


def take(x, ind, axis):
    other = 1 - axis
    dims = lax.GatherDimensionNumbers(
        offset_dims=(), collapsed_slice_dims=(axis,), start_index_map=(axis,),
        operand_batching_dims=(other,), start_indices_batching_dims=(other,))
    return lax.gather(x, ind[..., None], dims, slice_sizes=(1, 1),
                      mode=lax.GatherScatterMode.PROMISE_IN_BOUNDS)


def dot_nt(a, b):
    return lax.dot_general(a, b, (((1,), (1,)), ((), ())), preferred_element_type=F32)


def fold(gram):
    return jnp.concatenate([gram[:F // 2], gram[F // 2:]], axis=1)


def unfold(gram):
    return jnp.concatenate([gram[:, :F], gram[:, F:]], axis=0)


def make_table(x_ref, tab_ref, gram_ref):
    x = x_ref[...].astype(BF16)
    for h in range(x.shape[1] // LN):
        tab_ref[h * F:(h + 1) * F, :] = x[:, h * LN:(h + 1) * LN]
    gram_ref[...] = fold(dot_nt(x, x))


def code_weight(idx, conf):
    code = jnp.where(conf > 0.0, idx, EMPTY).astype(F32)
    return code, jnp.maximum(conf - 1.0, 0.0)


def arrange_users(me, idx_ref, conf_ref, out_ref, begin=0, end=None):
    skew = me % 16
    row, lane = iota((8, LN), 0), iota((8, LN), 1)
    first = (lane - 16 * row) & 127
    second = ((lane >> 4) - row) & 7
    third = ((lane ^ skew) + 16 * row) & 127
    dests = idx_ref.shape[1] // 512
    batch = min(8, dests)

    def arrange(x):
        return take(take(take(x, first, 1), second, 0), third, 1)

    def place(n, _):
        for e in range(batch):
            dest = n * batch + e
            owner = (dest // 32, dest // 8 % 4, dest // 2 % 4, dest % 2)
            codes = []
            for q in range(4):
                cols = pl.ds(pl.multiple_of(dest * 512 + q * LN, LN), LN)
                code, weight = code_weight(idx_ref[:, cols], conf_ref[:, cols])
                out_ref[(*owner, pl.ds(q * 8, 8), slice(None))] = arrange(weight)
                codes.append(arrange(code))
            for q in range(2):
                out_ref[(*owner, pl.ds(32 + q * 8, 8), slice(None))] = codes[q] + PACK * codes[q + 2]
        return 0

    lax.fori_loop(begin, dests // batch if end is None else end, place, 0)


def arrange_items(me, idx_ref, conf_ref, out_ref):
    skew = me % 64
    lane = iota((8, LN), 1)
    pattern = lane ^ skew
    low = lane < 64

    def halves(x0, x1):
        a = jnp.where(low, x0, pltpu.roll(x1, 64, 1))
        b = jnp.where(low, pltpu.roll(x0, 64, 1), x1)
        return take(a, pattern, 1), take(b, pattern, 1)

    def place(dest, _):
        for q in range(2):
            base = dest * 32 + q * 16
            rows = [pl.ds(base + j, 8, stride=2) for j in range(2)]
            pairs = [code_weight(idx_ref[r, :], conf_ref[r, :]) for r in rows]
            code_a, code_b = halves(pairs[0][0], pairs[1][0])
            weight_a, weight_b = halves(pairs[0][1], pairs[1][1])
            out_ref[dest, pl.ds(q * 8, 8), :] = weight_a
            out_ref[dest, pl.ds(16 + q * 8, 8), :] = weight_b
            out_ref[dest, pl.ds(32 + q * 8, 8), :] = code_a + PACK * code_b
        return 0

    lax.fori_loop(0, out_ref.shape[0], place, 0, unroll=min(8, out_ref.shape[0]))


ORDERS = ((2, 1, 0), (1, 0, 2), (0, 2, 1))
STRIDES = (32, 8, 2)
RING = 4


def gather_kernel(streams, beside_work, *refs):
    if beside_work:
        (rows_hbm, uidx_hbm, uconf_hbm, idx_hbm, conf_hbm, *outs, arrived, pay_hbm,
         send, recv, pass_send, pass_recv, local, uidx, uconf, idx, conf, pay, stage, relay,
         swap_send, swap_recv, work, table, gram, rows_ref) = refs
        loads = [pltpu.make_async_copy(a, b, work.at[n]) for n, (a, b) in enumerate(
            ((uidx_hbm, uidx), (uconf_hbm, uconf), (idx_hbm, idx), (conf_hbm, conf)))]
        firsts = [pltpu.make_async_copy(rows_hbm, rows_ref, work.at[6])]
    else:
        table_hbm, gram_hbm, *outs, send, recv, pass_send, pass_recv, local, table, gram, work = refs
        loads = []
        firsts = [pltpu.make_async_copy(table_hbm, table, work.at[0]), pltpu.make_async_copy(gram_hbm, gram, work.at[1])]
    for copy in firsts + loads:
        copy.start()
    ins = (table, gram)
    me = lax.axis_index('g')
    core = me % 2
    here = [me // stride % RING for stride in STRIDES]
    partner = me + 1 - 2 * core

    def beside(dim, delta):
        return me + ((here[dim] + delta + RING) % RING - here[dim]) * STRIDES[dim]

    barrier = pltpu.get_barrier_semaphore()
    peers = [beside(dim, delta) for dim in range(3) for delta in ((1, -1) if beside_work else (1, -1, 2))] + [partner]
    for peer in peers:
        pl.semaphore_signal(barrier, inc=1, device_id={'g': peer}, device_id_type=pl.DeviceIdType.MESH)
    for copy in firsts:
        copy.wait()
    if beside_work:
        make_table(rows_ref, table, gram)
    pl.semaphore_wait(barrier, len(peers))

    def region(s, phase, dim, delta, half):
        which, first, rows = streams[s][:3]
        order = ORDERS[streams[s][3]]
        index = []
        for d in range(3):
            if d in order[:phase]:
                index.append(pl.ds(0, RING))
            else:
                index.append((here[d] + delta + RING) % RING if d == dim else here[d])
        if half is not None:
            rows = rows // 2
            first = first + half * rows
        return outs[which].at[(*index, core, pl.ds(first, rows), slice(None))]

    def remote(src, dst, sems, index, peer):
        return pltpu.make_async_remote_copy(
            src_ref=src, dst_ref=dst, send_sem=sems[0].at[index], recv_sem=sems[1].at[index],
            device_id={'g': peer}, device_id_type=pl.DeviceIdType.MESH)

    swaps = {}

    def slab(level, dim, delta, color, half=None):
        index = [pl.ds(0, RING)] * 3
        index[dim] = (here[dim] + delta + RING) % RING
        rows = pl.ds(16 * color, 16) if half is None else pl.ds(16 * color + 8 * half, 8)
        return stage.at[(level, *index, pl.ds(0, 2), rows, slice(None))]

    def swap(src, dst, index, peer):
        copy = remote(src, dst, (swap_send, swap_recv), index, peer)
        copy.start()
        swaps[index] = copy

    def swap_start(phase):
        for color in range(3):
            dim = ORDERS[color][phase]
            base = (phase * 3 + color) * 6
            for way, delta in enumerate((1, -1)):
                swap(slab(phase, dim, delta, color), slab(phase + 1, dim, 0, color), base + way, beside(dim, delta))
                swap(slab(phase, dim, 2, color, way), relay.at[phase, color, way], base + 2 + way, beside(dim, delta))
        for color in range(3):
            dim = ORDERS[color][phase]
            index = [pl.ds(0, RING)] * 3
            index[dim] = pl.ds(here[dim], 1)
            part = (*index, pl.ds(0, 2), pl.ds(16 * color, 16), slice(None))
            stage[(phase + 1, *part)] = stage[(phase, *part)]

    def swap_further(phase):
        for color in range(3):
            dim = ORDERS[color][phase]
            base = (phase * 3 + color) * 6
            for way, delta in enumerate((1, -1)):
                swaps[base + 2 + way].wait_recv()
                swap(relay.at[phase, color, way], slab(phase + 1, dim, -delta, color, way), base + 4 + way, beside(dim, delta))

    def swap_finish(phase):
        for color in range(3):
            base = (phase * 3 + color) * 6
            for n in (0, 1, 4, 5):
                swaps[base + n].wait_recv()

    def swap_cores():
        everywhere = [pl.ds(0, RING)] * 3
        mine = arrived.at[(*everywhere, core)]
        swap(stage.at[(3, *everywhere, 1 - core)], mine, 54, partner)
        stay = pltpu.make_async_copy(stage.at[(3, *everywhere, core)], mine, work.at[4])
        stay.start()
        stay.wait()
        for copy in swaps.values():
            copy.wait_send()
        swaps[54].wait_recv()

    passed = {s: [] for s in range(len(streams))}

    def pass_on(src, dst, s, slot):
        copy = remote(src, dst, (pass_send, pass_recv), 13 * s + slot, partner)
        copy.start()
        passed[s].append(copy)

    count = len(streams)
    own, kept = [], []
    for s, (which, first, rows, _) in enumerate(streams):
        src = ins[which].at[pl.ds(first, rows), :]
        own.append(src)
        copy = pltpu.make_async_copy(src, region(s, 0, 0, 0, None), local.at[s])
        copy.start()
        kept.append(copy)
    sent, across, further = [], {}, {}

    def start_across(s, phase):
        dim = ORDERS[streams[s][3]][phase]
        for way, delta in enumerate((1, -1)):
            mine = region(s, phase, dim, 0, None)
            src = own[s] if phase == 0 else mine
            across[s, way] = remote(src, mine, (send, recv), ((s * 3 + phase) * 2 + 0) * 2 + way, beside(dim, delta))
            across[s, way].start()
            sent.append(across[s, way])
        if phase == 0 and not beside_work:
            opposite = remote(own[s], region(s, phase, dim, 0, None), (send, recv), (s * 3 * 2 + 1) * 2, beside(dim, 2))
            opposite.start()
            sent.append(opposite)
            further[s, 0] = opposite

    def start_further(s, phase):
        dim = ORDERS[streams[s][3]][phase]
        if phase == 0 and not beside_work:
            for way, delta in enumerate((1, -1)):
                across[s, way].wait_recv()
                whole = region(s, phase, dim, -delta, None)
                pass_on(whole, whole, s, 1 + way)
            return
        for way, delta in enumerate((1, -1)):
            across[s, way].wait_recv()
            half = region(s, phase, dim, -delta, way)
            further[s, way] = remote(half, half, (send, recv), ((s * 3 + phase) * 2 + 1) * 2 + way, beside(dim, delta))
            further[s, way].start()
            sent.append(further[s, way])
        for way, delta in enumerate((1, -1)):
            whole = region(s, phase, dim, -delta, None)
            pass_on(whole, whole, s, 1 + 4 * phase + way)

    def finish(s, phase):
        dim = ORDERS[streams[s][3]][phase]
        once = phase == 0 and not beside_work
        for way in range(1 if once else 2):
            further[s, way].wait_recv()
        if phase == 0:
            kept[s].wait()
        if phase < 2:
            start_across(s, phase + 1)
        for way in range(1 if once else 2):
            half = region(s, phase, dim, 2, None if once else way)
            pass_on(half, half, s, 3 + 4 * phase + way)

    for s in range(count):
        start_across(s, 0)
    for s in range(count):
        pass_on(own[s], region(s, 0, 0, 0, None), s, 0)

    def every(step, phase, part=slice(None)):
        for s in range(count)[part]:
            step(s, phase)

    early, late = slice(0, 4), slice(4, None)
    if beside_work:
        loads[0].wait()
        loads[1].wait()
        arrange_users(me, uidx, uconf, stage.at[0], 0, 8)
        every(start_further, 0)
        arrange_users(me, uidx, uconf, stage.at[0], 8, 16)
        every(finish, 0)
        swap_start(0)
        every(start_further, 1)
        every(finish, 1, early)
        swap_further(0)
        swap_finish(0)
        swap_start(1)
        every(finish, 1, late)
        loads[2].wait()
        loads[3].wait()
        arrange_items(me, idx, conf, pay)
        swap_further(1)
        swap_finish(1)
        swap_start(2)
        every(start_further, 2, early)
        store = pltpu.make_async_copy(pay, pay_hbm, work.at[5])
        store.start()
        swap_further(2)
        every(start_further, 2, late)
        swap_finish(2)
        every(finish, 2)
        swap_cores()
        store.wait()
    else:
        for phase in range(3):
            every(start_further, phase)
            every(finish, phase)
    for copy in sent:
        copy.wait_send()
    for s in range(count):
        for copy in passed[s]:
            copy.wait_send()
    for s in range(count):
        for copy in passed[s]:
            copy.wait_recv()


def gather_all(sources, shapes, collective_id, slots=()):
    table, gram = shapes
    rows = table.shape[0]
    units = rows // 16
    parts = 3 if slots else 2
    share = (units + 4) // 3
    totals = (share, share, units - 2 * share)
    sizes = [total // parts + (n < total % parts) for n in range(parts) for total in totals]
    streams, first = [(1, 0, gram.shape[0], 2)], 0
    for n, size in enumerate(sizes):
        streams.append((0, first, 16 * size, n % 3))
        first += 16 * size
    count = len(streams)
    any_spec = pl.BlockSpec(memory_space=pl.ANY)
    out_shape = [jax.ShapeDtypeStruct((RING, RING, RING, 2, *x.shape), x.dtype) for x in shapes]
    scratch = [pltpu.SemaphoreType.DMA((12 * count,)), pltpu.SemaphoreType.DMA((12 * count,)),
               pltpu.SemaphoreType.DMA((13 * count,)), pltpu.SemaphoreType.DMA((13 * count,)),
               pltpu.SemaphoreType.DMA((count,))]
    if slots:
        blocks = (RING, RING, RING, 2, PAY, LN)
        out_shape += [jax.ShapeDtypeStruct(blocks, F32), jax.ShapeDtypeStruct((G, PAY, LN), F32)]
        scratch += [pltpu.VMEM(x.shape, x.dtype) for x in slots]
        scratch += [pltpu.VMEM((G, PAY, LN), F32), pltpu.VMEM((4, *blocks), F32),
                    pltpu.VMEM((3, 3, 2, RING, RING, 2, 8, LN), F32),
                    pltpu.SemaphoreType.DMA((55,)), pltpu.SemaphoreType.DMA((55,)), pltpu.SemaphoreType.DMA((7,)),
                    pltpu.VMEM(table.shape, table.dtype), pltpu.VMEM(gram.shape, gram.dtype),
                    pltpu.VMEM(sources[0].shape, F32)]
    else:
        scratch += [pltpu.VMEM(table.shape, table.dtype), pltpu.VMEM(gram.shape, gram.dtype), pltpu.SemaphoreType.DMA((2,))]
    tables, grams, *payload = pl.pallas_call(
        functools.partial(gather_kernel, tuple(streams), bool(slots)),
        in_specs=[any_spec] * (len(sources) + len(slots)),
        out_specs=[any_spec] * len(out_shape),
        out_shape=out_shape,
        scratch_shapes=scratch,
        compiler_params=pltpu.CompilerParams(collective_id=collective_id, has_side_effects=True),
        name='gather_all',
    )(*sources, *slots)
    return tables.reshape(G, -1, F, LN), grams.reshape(-1, LN), *payload


def half_kernel(slots, blocks, pair, lanes_of, body, emit, tab_hbm, pay_hbm, gram_hbm, x0_hbm, *refs):
    if emit:
        out_ref, tab_ref, gout_ref = refs[:3]
        refs = refs[3:]
    else:
        out_ref = refs[0]
        refs = refs[1:]
    tab, pay, ids, yu_a, yu_b, wu_a, wu_b, a_scr, at_scr, p_scr, s_scr, gpad_ref, gram_ref, x0_ref, sems = refs
    per = LN // slots
    chunks = G // per
    groups = LN // per
    steps = blocks * groups // pair
    turns = groups // pair
    heads = tab.shape[1]

    pay_copy = pltpu.make_async_copy(pay_hbm, pay, sems.at[8])
    pay_copy.start()

    def tab_copy(i):
        return pltpu.make_async_copy(tab_hbm.at[pl.ds(16 * i, 16)], tab.at[pl.ds(16 * i, 16)], sems.at[i])

    for i in range(8):
        tab_copy(i).start()
    side_copies = [pltpu.make_async_copy(gram_hbm, gram_ref, sems.at[9]), pltpu.make_async_copy(x0_hbm, x0_ref, sems.at[10])]
    for copy in side_copies:
        copy.start()
    ids[...] = iota((2 * LN, LN), 0, I16)
    pay_copy.wait()

    lane16 = iota((16, LN), 1, I16)
    lane = iota((8, LN), 1)
    row = iota((8, LN), 0)

    def sum_grams():
        for copy in side_copies:
            copy.wait()

        def add_gram(d, acc):
            return acc + gram_ref[pl.ds(pl.multiple_of(d * (F // 2), F // 2), F // 2), :]

        gram = lax.fori_loop(0, G, add_gram, jnp.zeros((F // 2, LN), F32), unroll=8)
        gpad = jnp.concatenate([unfold(gram), jnp.zeros((16, F), F32)], axis=0)
        gpad = jnp.concatenate([gpad, jnp.zeros((FX, 16), F32)], axis=1)
        rr, cc = iota((FX, FX), 0), iota((FX, FX), 1)
        gpad_ref[...] = gpad + jnp.where((rr == cc) & (rr < F), REG_LAMBDA, 0.0)

    def pay_row(t):
        if slots == 8:
            return t, 32 + t % 16, 12 * (t // 16)
        return (t % 2) * 16 + t // 2, 32 + t // 2, 12 * (t % 2)

    def spread_weights(t, wu, q):
        wrow = pay_row(t)[0]
        for c in range(chunks):
            tiles = []
            for v in range(per // 8):
                start = (per * c + 8 * v) * PAY + wrow
                tiles.append(pay[pl.ds(start, 8, stride=PAY), :])
            for bit in (1, 2, 4):
                hit = (lane & bit) != 0
                up = (row & bit) != 0
                for v in range(len(tiles)):
                    x = tiles[v]
                    if bit == 4:
                        other = pltpu.roll(x, 4, 0)
                    else:
                        other = jnp.where(up, pltpu.roll(x, bit, 0), pltpu.roll(x, 8 - bit, 0))
                    tiles[v] = jnp.where(hit, other, x)
            bit = 8
            while bit < per:
                hit = (lane & bit) != 0
                tiles = [jnp.where(hit, tiles[v ^ (bit // 8)], tiles[v]) for v in range(len(tiles))]
                bit *= 2
            for v in range(len(tiles)):
                wu[c, pl.ds(per * q + 8 * v, 8), :] = tiles[v]

    def exchange(xs, low_bit):
        bit, n = 1, len(xs)
        while bit < n:
            hit = (lane16 & I16(bit * low_bit)) != I16(0)
            xs = [jnp.where(hit, xs[a ^ bit], xs[a]) for a in range(n)]
            bit *= 2
        return xs

    ones = jnp.ones((16, LN * chunks), BF16)

    def form(y_parts, wu, u, at):
        vs = []
        for c in range(chunks):
            w = wu[c, pl.ds(u, 1), :]
            vs.append((y_parts[c].astype(F32) * w).astype(BF16))
        y = jnp.concatenate([jnp.concatenate(y_parts, axis=1), ones], axis=0)
        v = jnp.concatenate([jnp.concatenate(vs, axis=1), ones], axis=0)
        a_scr[pl.ds(at * PITCH, PITCH), pl.ds(0, FX)] = (dot_nt(y, v) + gpad_ref[...])[:PITCH]

    def form_rows(t, i, yu, wu):
        first = (t - 1) // turns % 2 * LN + (t - 1) % turns * (per * pair)
        rows = [per * (i // 4) + i % 4 + 4 * m for m in range(per // 4)]
        parts = []
        for c in range(chunks):
            by_k = [exchange([yu[u, c, pl.ds(16 * k, 16), :] for u in rows], 4) for k in range(4)]
            parts.append([jnp.concatenate([x[m] for x in by_k], axis=0) for m in range(len(rows))])
        for m, u in enumerate(rows):
            form([parts[c][m] for c in range(chunks)], wu, u, first + u)

    def codes(t, d, q):
        _, crow, shift = pay_row(pair * t + q)
        packed = pay[pl.ds(d * PAY + crow, 1), :].astype(I32)
        return (packed >> shift) & (PACK - 1)

    def by_lanes(t, d, q):
        code = jnp.broadcast_to(codes(t, d, q), (F, LN)).astype(I16)
        low = code & I16(LN - 1)
        head = code >> I16(7)
        acc = jnp.zeros((F, LN), BF16)
        for h in range(heads):
            acc = jnp.where(head == I16(h), take(tab[d, h], low, 1), acc)
        return acc

    def by_matmul(t, d):
        hots, halves = [], []
        for q in range(2):
            code = codes(t, d, q)
            low = (jnp.broadcast_to(code, (2 * LN, LN)) & (2 * LN - 1)).astype(I16)
            hots.append(jnp.where(low == ids[...], jnp.ones((2 * LN, LN), BF16), jnp.zeros((2 * LN, LN), BF16)))
            halves.append(jnp.broadcast_to(code, (F, LN)) >> 8)
        table = jnp.concatenate([jnp.concatenate([tab[d, 2 * h], tab[d, 2 * h + 1]], axis=1)
                                 for h in range(heads // 2)], axis=0)
        found = jnp.dot(table, jnp.concatenate(hots, axis=1), preferred_element_type=F32)
        out = []
        for q in range(2):
            acc = jnp.zeros((F, LN), F32)
            for h in range(heads // 2):
                acc = jnp.where(halves[q] == h, found[h * F:(h + 1) * F, q * LN:(q + 1) * LN], acc)
            out.append(acc.astype(BF16))
        return out

    def lookup(t, i, yu):
        for quad in range(4):
            found = []
            for dd in range(4):
                d = 16 * i + 4 * quad + dd
                if 4 * quad + dd < lanes_of:
                    found.append([by_lanes(t, d, q) for q in range(pair)])
                else:
                    found.append(by_matmul(t, d))
            for q in range(pair):
                for k in range(4):
                    rows = slice(16 * k, 16 * k + 16)
                    xs = exchange([x[q][rows] for x in found], 1)
                    for a in range(4):
                        if slots == 8:
                            yu[16 * q + 4 * quad + a, i, rows, :] = xs[a]
                        else:
                            yu[64 * q + (i % 4) * 16 + 4 * quad + a, i // 4, rows, :] = xs[a]

    def flip(block, b):
        m = a_scr[pl.ds(block % 2 * (LN * PITCH) + b, LN, stride=PITCH), :].T
        at_scr[b] = m[:F]
        s_scr[pl.ds(b, 1), :] = m[F:F + 1]

    def flip_all(block):
        def four(b4, _):
            for e in range(4):
                flip(block, 4 * b4 + e)
            return 0

        lax.fori_loop(0, F // 4, four, 0)

    def solve(block):
        rhs = a_scr[pl.ds(block % 2 * (LN * PITCH) + F, LN, stride=PITCH), :].T[:F] + s_scr[...]
        x = x0_ref[:, pl.ds(pl.multiple_of(block * LN, LN), LN)]

        def apply_mat(vec):
            p_scr[...] = vec

            def add(b, acc):
                return acc + at_scr[b] * p_scr[pl.ds(b, 1), :]

            return lax.fori_loop(0, F, add, jnp.zeros((F, LN), F32), unroll=16)

        res = rhs - apply_mat(x)
        direction = res
        res_sq = jnp.sum(res * res, axis=0, keepdims=True)
        for step in range(CG_STEPS):
            q = apply_mat(direction)
            length = res_sq / jnp.sum(direction * q, axis=0, keepdims=True)
            x = x + length * direction
            if step + 1 < CG_STEPS:
                res = res - length * q
                new_sq = jnp.sum(res * res, axis=0, keepdims=True)
                direction = res + (new_sq / res_sq) * direction
                res_sq = new_sq
        out_ref[:, pl.ds(pl.multiple_of(block * LN, LN), LN)] = x
        if emit:
            xb = x.astype(BF16)
            tab_ref[block] = xb
            gout_ref[...] += fold(dot_nt(xb, xb))

    if emit:
        gout_ref[...] = jnp.zeros((F // 2, LN), F32)

    def weights(t, wu):
        for q in range(pair):
            spread_weights(pair * t + q, wu, q)

    def first_pass():
        weights(0, wu_a)

        def inner(i, _):
            tab_copy(i).wait()
            lookup(0, i, yu_a)
            return 0

        lax.fori_loop(0, 8, inner, 0)

    def step_pass(t, ahead, count, size, yu, wu, yu_last, wu_last):
        before = jnp.maximum((t - 1) // turns - 1, 0)
        if ahead:
            weights(jnp.minimum(t, steps - 1), wu)

        def inner(i2, _):
            flips = F // (8 * turns)
            for i in range(size):
                i = size * i2 + i
                for e in range(flips):
                    flip(before, ((t - 1) % turns * 8 + i) * flips + e)
                jobs = [functools.partial(form_rows, t, i, yu_last, wu_last)]
                if ahead:
                    jobs.insert(0 if body > 1 else 1, functools.partial(lookup, t, i, yu))
                for job in jobs:
                    job()
            return 0

        lax.fori_loop(0, count, inner, 0)

        def finish_block():
            @pl.when((t >= turns + 1) & (t % turns == 0))
            def _():
                solve(t // turns - 2)

        if ahead:
            pl.when(t < steps)(finish_block)
        else:
            finish_block()

    def two_steps(j, _):
        step_pass(2 * j + 1, True, 8 // body, body, yu_b, wu_b, yu_a, wu_a)
        step_pass(2 * j + 2, True, jnp.where(2 * j + 2 < steps, 8 // body, 0), body, yu_a, wu_a, yu_b, wu_b)
        return 0

    first_pass()
    sum_grams()
    lax.fori_loop(0, steps // 2, two_steps, 0)
    step_pass(steps, False, 8, 1, None, None, yu_b, wu_b)
    flip_all(blocks - 1)
    solve(blocks - 1)


def half_step(slots, emit, pair, lanes_of, body, tables, payload, gram, x0_t):
    n = x0_t.shape[1]
    heads = tables.shape[1]
    per = LN // slots
    chunks = G // per
    out_shape = [jax.ShapeDtypeStruct((F, n), F32)]
    if emit:
        out_shape += [jax.ShapeDtypeStruct((n // LN, F, LN), BF16), jax.ShapeDtypeStruct((F // 2, LN), F32)]
    vmem = pl.BlockSpec(memory_space=pltpu.VMEM)
    return pl.pallas_call(
        functools.partial(half_kernel, slots, n // LN, pair, lanes_of, body, emit),
        in_specs=[pl.BlockSpec(memory_space=pl.ANY)] * 4,
        out_specs=[vmem] * len(out_shape),
        out_shape=out_shape,
        scratch_shapes=[
            pltpu.VMEM((G, heads, F, LN), BF16),
            pltpu.VMEM((G * PAY, LN), F32),
            pltpu.VMEM((2 * LN, LN), I16),
            pltpu.VMEM((pair * per, chunks, F, LN), BF16),
            pltpu.VMEM((pair * per, chunks, F, LN), BF16),
            pltpu.VMEM((chunks, pair * per, LN), F32),
            pltpu.VMEM((chunks, pair * per, LN), F32),
            pltpu.VMEM((2 * LN * PITCH, LN), F32),
            pltpu.VMEM((F, F, LN), F32),
            pltpu.VMEM((F, LN), F32),
            pltpu.VMEM((F, LN), F32),
            pltpu.VMEM((FX, FX), F32),
            pltpu.VMEM(gram.shape, F32),
            pltpu.VMEM(x0_t.shape, F32),
            pltpu.SemaphoreType.DMA((11,)),
        ],
        compiler_params=pltpu.CompilerParams(vmem_limit_bytes=62 * 1024 * 1024),
        cost_estimate=pl.CostEstimate(flops=10 ** 11, bytes_accessed=2 ** 25, transcendentals=0),
        name='half_step',
    )(tables, payload, gram, x0_t)


def solution(mesh):
    part_spec = P(('tables', 'g'), None)
    slot_spec = P(('tables', 'g'), None, None)

    def local_sweep(item_block, start_block, item_idx, item_conf, user_idx, user_conf):
        item_t = item_block.T

        def as_rows(x):
            return x[0].reshape(-1, LN, 2).transpose(0, 2, 1).reshape(-1, LN)

        gram_shape = jax.ShapeDtypeStruct((F // 2, LN), F32)
        tables, gram_items, payload, late = gather_all(
            (item_t,), (jax.ShapeDtypeStruct((item_t.size // LN, LN), BF16), gram_shape), 0,
            (item_idx[0].T, item_conf[0].T, as_rows(user_idx), as_rows(user_conf)))
        late = lax.all_to_all(late, 'g', 0, 0, tiled=True)
        user_t, user_table, gram_part = half_step(8, True, 2, 6, 2, tables, payload.reshape(G * PAY, LN),
                                                  gram_items, start_block.T)
        user_table = user_table.reshape(-1, LN)
        user_tables, gram_users = gather_all((user_table, gram_part), (user_table, gram_part), 1)
        item_new = half_step(2, False, 2, 6, 1, user_tables, late.reshape(G * PAY, LN), gram_users, item_t)[0]
        return user_t.T, item_new.T

    return jax.shard_map(local_sweep, mesh=mesh,
                         in_specs=(part_spec, part_spec, slot_spec, slot_spec, slot_spec, slot_spec),
                         out_specs=(part_spec, part_spec), check_vma=False)
```

profile of v0, /device:TPU:1, one launch (start us, length us, event | category | flops | bytes accessed | tf_op | source)
XLA Modules:
  0.0 434.2 jit_solution(7171984806852529804)
XLA Ops:
  0.6 125.3 %gather_all.2 = (bf16[4,4,4,2,1024,128]{5,4,3,2,1,0:T(8,128)(2,1)}, f32[4,4,4,2,32,128]{5,4,3,2,1,0:T(8,128)}, f32[4,4,4,2,48,128]{5,4,3,2,1,0:T(8,128)}, f32[128,48,128]{2,1,0:T(8,128)}) custom-call(f32[64,2048]{1,0:T(8,128)} %bitcast.31, s32[8,65536]{1,0:T(8,128)} %bitcast.27, f32[8,65536]{1,0:T(8,128)} %bitcast.28, s32[4096,128]{1,0:T(8,128)} %bitcast.29, ...), custom_call_target="tpu_custom_call" | custom-call | tf_op jit(solution)/shard_map/gather_all/pallas_call | solution.py:372
  125.9 5.2 %all-to-all-start = ((f32[128,48,128]{2,1,0:T(8,128)}), f32[128,48,128]{2,1,0:T(8,128)}, u32[]{:S(2)}, u32[]{:S(2)}) async-start(f32[128,48,128]{2,1,0:T(8,128)} %get-tuple-element.18), calls=%async_computation | async-start | bytes 6291456 | tf_op jit(solution)/shard_map/all_to_all | solution.py:694
  131.1 155.9 %half_step.2 = (f32[64,512]{1,0:T(8,128)}, bf16[4,64,128]{2,1,0:T(8,128)(2,1)}, f32[32,128]{1,0:T(8,128)}) custom-call(bf16[128,16,64,128]{3,2,1,0:T(8,128)(2,1)} %bitcast.34, f32[6144,128]{1,0:T(8,128)} %bitcast.36, f32[4096,128]{1,0:T(8,128)} %bitcast.37, f32[64,512]{1,0:T(8,128)} %bitcast.39), custom_call_target="tpu_custom_call" | custom-call | flops 99999997952 | bytes 33554432 | tf_op jit(solution)/shard_map/half_step/pallas_call | solution.py:652
  287.1 39.9 %gather_all.3 = (bf16[4,4,4,2,256,128]{5,4,3,2,1,0:T(8,128)(2,1)}, f32[4,4,4,2,32,128]{5,4,3,2,1,0:T(8,128)}) custom-call(bf16[256,128]{1,0:T(8,128)(2,1)} %bitcast.33, f32[32,128]{1,0:T(8,128)} %get-tuple-element.16.refs_1_), custom_call_target="tpu_custom_call" | custom-call | tf_op jit(solution)/shard_map/gather_all/pallas_call | solution.py:372
  327.0 0.0 all-to-all-done
  327.0 107.0 %half_step.3 = f32[64,2048]{1,0:T(8,128)} custom-call(bf16[128,4,64,128]{3,2,1,0:T(8,128)(2,1)} %bitcast.35, f32[6144,128]{1,0:T(8,128)} %bitcast.18.pay_hbm, f32[4096,128]{1,0:T(8,128)} %bitcast.38, f32[64,2048]{1,0:T(8,128)} %bitcast.32), custom_call_target="tpu_custom_call" | custom-call | flops 99999997952 | bytes 33554432 | tf_op jit(solution)/shard_map/half_step/pallas_call | solution.py:652
Async XLA Ops:
  125.9 201.1 %all-to-all-start = ((f32[128,48,128]{2,1,0:T(8,128)}), f32[128,48,128]{2,1,0:T(8,128)}, u32[]{:S(2)}, u32[]{:S(2)}) async-start(f32[128,48,128]{2,1,0:T(8,128)} %get-tuple-element.18), calls=%async_computation | async-start | bytes 6291456 | tf_op jit(solution)/shard_map/all_to_all | solution.py:694
where the time goes:
time: 434 us
  Pallas kernels  428 us (99%)
  starting transfers between devices  5.19 us (1%)
    pallas_call x2, Pallas kernels, half_step(): pl.pallas_call(functools.partial(half_kernel, slots, n // LN, pair, lanes...  263 us
    pallas_call x2, Pallas kernels, gather_all(): pl.pallas_call(functools.partial(gather_kernel, tuple(streams), bool(slot...  165 us
  transfers between devices with their start and end apart: 1, of which 0 were waited for; matrix products, arithmetic and copies ran while one was open for 0% of the time, Pallas kernels for 45%

commit v1 on v0

--- a/solution.py
+++ b/solution.py
@@ -522,8 +522,9 @@
         for quad in range(4):
             found = []
             for dd in range(4):
-                d = 16 * i + 4 * quad + dd
-                if 4 * quad + dd < lanes_of:
+                n = 4 * quad + dd
+                d = 16 * i + n
+                if (n + 1) * lanes_of // 16 > n * lanes_of // 16 if slots == 8 else n < lanes_of:
                     found.append([by_lanes(t, d, q) for q in range(pair)])
                 else:
                     found.append(by_matmul(t, d))

time: 434 us -> 434 us (level)
  no operation moved by 1% of the time
where the time goes in v1:
time: 434 us; the launch traced here: 433 us
  Pallas kernels  427 us (98%)
  starting transfers between devices  5.19 us (1%)
    pallas_call x2, Pallas kernels, half_step(): pl.pallas_call(functools.partial(half_kernel, slots, n // LN, pair, lanes...  262 us
    pallas_call x2, Pallas kernels, gather_all(): pl.pallas_call(functools.partial(gather_kernel, tuple(streams), bool(slot...  165 us
  transfers between devices with their start and end apart: 1, of which 0 were waited for; matrix products, arithmetic and copies ran while one was open for 0% of the time, Pallas kernels for 45%

profile of v1, /device:TPU:1, one launch (start us, length us, event | category | flops | bytes accessed | tf_op | source)
XLA Modules:
  0.0 433.3 jit_solution(7403823874970560579)
XLA Ops:
  0.6 125.3 %gather_all.2 = (bf16[4,4,4,2,1024,128]{5,4,3,2,1,0:T(8,128)(2,1)}, f32[4,4,4,2,32,128]{5,4,3,2,1,0:T(8,128)}, f32[4,4,4,2,48,128]{5,4,3,2,1,0:T(8,128)}, f32[128,48,128]{2,1,0:T(8,128)}) custom-call(f32[64,2048]{1,0:T(8,128)} %bitcast.31, s32[8,65536]{1,0:T(8,128)} %bitcast.27, f32[8,65536]{1,0:T(8,128)} %bitcast.28, s32[4096,128]{1,0:T(8,128)} %bitcast.29, ...), custom_call_target="tpu_custom_call" | custom-call | tf_op jit(solution)/shard_map/gather_all/pallas_call | solution.py:372
  125.9 5.2 %all-to-all-start = ((f32[128,48,128]{2,1,0:T(8,128)}), f32[128,48,128]{2,1,0:T(8,128)}, u32[]{:S(2)}, u32[]{:S(2)}) async-start(f32[128,48,128]{2,1,0:T(8,128)} %get-tuple-element.18), calls=%async_computation | async-start | bytes 6291456 | tf_op jit(solution)/shard_map/all_to_all | solution.py:695
  131.1 155.0 %half_step.2 = (f32[64,512]{1,0:T(8,128)}, bf16[4,64,128]{2,1,0:T(8,128)(2,1)}, f32[32,128]{1,0:T(8,128)}) custom-call(bf16[128,16,64,128]{3,2,1,0:T(8,128)(2,1)} %bitcast.34, f32[6144,128]{1,0:T(8,128)} %bitcast.36, f32[4096,128]{1,0:T(8,128)} %bitcast.37, f32[64,512]{1,0:T(8,128)} %bitcast.39), custom_call_target="tpu_custom_call" | custom-call | flops 99999997952 | bytes 33554432 | tf_op jit(solution)/shard_map/half_step/pallas_call | solution.py:653
  286.1 40.0 %gather_all.3 = (bf16[4,4,4,2,256,128]{5,4,3,2,1,0:T(8,128)(2,1)}, f32[4,4,4,2,32,128]{5,4,3,2,1,0:T(8,128)}) custom-call(bf16[256,128]{1,0:T(8,128)(2,1)} %bitcast.33, f32[32,128]{1,0:T(8,128)} %get-tuple-element.16.refs_1_), custom_call_target="tpu_custom_call" | custom-call | tf_op jit(solution)/shard_map/gather_all/pallas_call | solution.py:372
  326.1 0.0 all-to-all-done
  326.1 107.0 %half_step.3 = f32[64,2048]{1,0:T(8,128)} custom-call(bf16[128,4,64,128]{3,2,1,0:T(8,128)(2,1)} %bitcast.35, f32[6144,128]{1,0:T(8,128)} %bitcast.18.pay_hbm, f32[4096,128]{1,0:T(8,128)} %bitcast.38, f32[64,2048]{1,0:T(8,128)} %bitcast.32), custom_call_target="tpu_custom_call" | custom-call | flops 99999997952 | bytes 33554432 | tf_op jit(solution)/shard_map/half_step/pallas_call | solution.py:653
Async XLA Ops:
  125.9 200.2 %all-to-all-start = ((f32[128,48,128]{2,1,0:T(8,128)}), f32[128,48,128]{2,1,0:T(8,128)}, u32[]{:S(2)}, u32[]{:S(2)}) async-start(f32[128,48,128]{2,1,0:T(8,128)} %get-tuple-element.18), calls=%async_computation | async-start | bytes 6291456 | tf_op jit(solution)/shard_map/all_to_all | solution.py:695
